TPU v7x, 32 devices: a whole 2x2x4 slice. The times are simulated.
32 devices in a mesh: seq: 4 (over x, core), tensor: 8 (over z, y).
Axes of the slice: x: 2, y: 2, z: 4, core: 2. Of those that a mesh axis runs over, the one named last changes fastest.
Arguments:
- token_ids: int32 [2, 7], replicated, may hold values from 0 to 131071
- cache_lengths: int32 [7], replicated, may hold values from 1 to 5118
- embed_table: bfloat16 [131072, 1024], P('seq', 'tensor'), may hold values from -64 to 64
- attn_gain: float32 [1024], replicated, may hold values from 0.1 to 1.9
- final_gain: float32 [1024], replicated, may hold values from 0.1 to 1.9
- w_qkv: bfloat16 [1024, 3, 1024], P(None, None, 'tensor'), may hold values from -0.1875 to 0.1875
- w_out: bfloat16 [1024, 1024], P('tensor'), may hold values from -0.1875 to 0.1875
- cache_keys: bfloat16 [7, 5120, 1024], P(None, 'seq', 'tensor'), may hold values from -300 to 300
- cache_values: bfloat16 [7, 5120, 1024], P(None, 'seq', 'tensor'), may hold values from -24 to 24
Outputs:
- hidden: bfloat16 [2, 7, 1024], P(None, None, 'tensor')
- new_kv: bfloat16 [2, 2, 7, 1024], P(None, None, None, 'tensor')
- logprobs: float32 [2, 7, 131072], P(None, None, ('seq', 'tensor'))
All inputs are finite; a program needn't handle non-finite values.
Results may differ from a plain program's by a relative error of at most 0.0085.
The roundings to bfloat16 on the way count: a program that leaves them out, or rounds other values in their place, can miss the bound.
Values may be sent and summed in bfloat16 or wider, within the bound.
A program may use at most 64 MiB of HBM per device.

v0:
```python
import math
import jax
import jax.numpy as jnp
from jax import lax
from jax.sharding import PartitionSpec as P

HD = 128
epsilon = 1e-05
logit_gain = 2.0


def combined_all(value, axis, join):
    pieces = jax.tree.map(lambda part: lax.all_gather(part, axis), value)
    head = jax.tree.map(lambda part: part[0], pieces)
    tail = jax.tree.map(lambda part: part[1:], pieces)
    running, _ = lax.scan(lambda running, share: (join(running, share), None), head, tail)
    return running


def rotate(vector, positions):
    half_size = vector.shape[-1] // 2
    frequency = 10000.0 ** (-(jnp.arange(half_size, dtype=jnp.float32) * 2.0 / vector.shape[-1]))
    angles = positions.astype(jnp.float32)[..., None] * frequency
    cosine_term = jnp.cos(angles)[:, :, None, :]
    sine_term = jnp.sin(angles)[:, :, None, :]
    first_half = vector[..., :half_size]
    second_half = vector[..., half_size:]
    return jnp.concatenate(
        [
            first_half * cosine_term - second_half * sine_term,
            first_half * sine_term + second_half * cosine_term,
        ],
        -1,
    )


def pair_join(earlier, later):
    highest = jnp.maximum(earlier[0], later[0])
    return (
        highest,
        earlier[1] * jnp.exp(earlier[0] - highest) + later[1] * jnp.exp(later[0] - highest),
    )


def body(
    token_ids,
    cache_lengths,
    embed_table,
    attn_gain,
    final_gain,
    w_qkv,
    w_out,
    cache_keys,
    cache_values,
):
    streams = token_ids.shape[1]
    vocab_rows, local_width = embed_table.shape
    model_width = attn_gain.shape[0]
    heads_here = local_width // HD
    slot_count = cache_keys.shape[1]
    seq_index = lax.axis_index("seq")
    tensor_index = lax.axis_index("tensor")
    local_ids = token_ids - seq_index * vocab_rows
    inside = (local_ids >= 0) & (local_ids < vocab_rows)
    picked = embed_table[jnp.clip(local_ids, 0, vocab_rows - 1)]
    picked = jnp.where(inside[..., None], picked, jnp.zeros_like(picked))
    embed_local = lax.psum(picked.astype(jnp.float32).astype(jnp.bfloat16), "seq").astype(
        jnp.float32
    )
    embed_whole = lax.all_gather(
        embed_local.astype(jnp.bfloat16), "tensor", axis=2, tiled=True
    ).astype(jnp.float32)
    normed = (
        embed_whole
        * lax.rsqrt(jnp.mean(embed_whole * embed_whole, -1, keepdims=True) + epsilon)
        * attn_gain
    ).astype(jnp.bfloat16)
    projected = jnp.einsum("sbd,dcf->sbcf", normed, w_qkv, preferred_element_type=jnp.float32)
    head_shape = (2, streams, heads_here, HD)
    positions = cache_lengths[None, :] + jnp.arange(2, dtype=jnp.int32)[:, None]
    queries = rotate(projected[:, :, 0].reshape(head_shape), positions).astype(jnp.bfloat16)
    new_keys = rotate(projected[:, :, 1].reshape(head_shape), positions).astype(jnp.bfloat16)
    new_values = projected[:, :, 2].reshape(head_shape).astype(jnp.bfloat16)
    new_kv = jnp.stack(
        [new_keys.reshape(2, streams, local_width), new_values.reshape(2, streams, local_width)]
    )
    inverse = HD ** (-0.5)
    key_rows = cache_keys.reshape(streams, slot_count, heads_here, HD)
    value_rows = cache_values.reshape(streams, slot_count, heads_here, HD)
    scores = (
        jnp.einsum("sbhe,bjhe->sbhj", queries, key_rows, preferred_element_type=jnp.float32)
        * inverse
    )
    slot_positions = seq_index * slot_count + jnp.arange(slot_count, dtype=jnp.int32)
    visible = (slot_positions[None, :] < cache_lengths[:, None])[None, :, None, :]
    local_max = jnp.max(jnp.where(visible, scores, -1e30), -1)
    weights = jnp.where(visible, jnp.exp(scores - local_max[..., None]), 0.0)
    local_sum = jnp.sum(weights, -1)
    local_out = jnp.einsum(
        "sbhj,bjhe->sbhe",
        weights,
        value_rows,
        preferred_element_type=jnp.float32,
        precision=lax.Precision.HIGHEST,
    )
    highest = lax.pmax(local_max, "seq")
    factor = jnp.exp(local_max - highest)
    cache_total, cache_out = lax.psum((local_sum * factor, local_out * factor[..., None]), "seq")
    fresh_scores = (
        jnp.einsum("sbhe,tbhe->sbht", queries, new_keys, preferred_element_type=jnp.float32)
        * inverse
    )
    allowed = (jnp.arange(2)[None, :] <= jnp.arange(2)[:, None])[:, None, None, :]
    fresh_max = jnp.max(jnp.where(allowed, fresh_scores, -1e30), -1)
    overall = jnp.maximum(highest, fresh_max)
    fresh_weights = jnp.where(allowed, jnp.exp(fresh_scores - overall[..., None]), 0.0)
    cache_scale = jnp.exp(highest - overall)
    denominator = cache_total * cache_scale + jnp.sum(fresh_weights, -1)
    numerator = cache_out * cache_scale[..., None] + jnp.einsum(
        "sbht,tbhe->sbhe",
        fresh_weights,
        new_values,
        preferred_element_type=jnp.float32,
        precision=lax.Precision.HIGHEST,
    )
    attended = (
        (numerator / denominator[..., None]).astype(jnp.bfloat16).reshape(2 * streams, local_width)
    )
    mixed_rows = jnp.dot(attended, w_out, preferred_element_type=jnp.float32).reshape(
        2, streams, model_width
    )
    mixed_local = lax.psum_scatter(mixed_rows, "tensor", scatter_dimension=2, tiled=True)
    hidden = (embed_local + mixed_local).astype(jnp.bfloat16)
    hidden_float = hidden.astype(jnp.float32)
    final_squares = lax.psum(jnp.sum(hidden_float * hidden_float, -1), "tensor")
    factor_rows = (
        lax.rsqrt(final_squares / model_width + epsilon) * (logit_gain / math.sqrt(model_width))
    ).reshape(2 * streams, 1)
    final_local = lax.dynamic_slice_in_dim(final_gain, tensor_index * local_width, local_width)
    gated_rows = (hidden_float * final_local).astype(jnp.bfloat16).reshape(2 * streams, local_width)
    partial_logits = lax.dot_general(
        gated_rows, embed_table, (((1,), (1,)), ((), ())), preferred_element_type=jnp.float32
    )
    shares = (
        lax.psum_scatter(partial_logits, "tensor", scatter_dimension=1, tiled=True) * factor_rows
    )
    share_max = jnp.max(shares, -1)
    share_sum = jnp.sum(jnp.exp(shares - share_max[:, None]), -1)
    vocab_max, vocab_sum = combined_all((share_max, share_sum), ("seq", "tensor"), pair_join)
    logprobs = shares - (vocab_max + jnp.log(vocab_sum))[:, None]
    return (hidden, new_kv, logprobs.reshape(2, streams, -1))


def solution(mesh):
    in_specs = (
        P(),
        P(),
        P("seq", "tensor"),
        P(),
        P(),
        P(None, None, "tensor"),
        P("tensor", None),
        P(None, "seq", "tensor"),
        P(None, "seq", "tensor"),
    )
    out_specs = (
        P(None, None, "tensor"),
        P(None, None, None, "tensor"),
        P(None, None, ("seq", "tensor")),
    )
    return jax.shard_map(body, mesh=mesh, in_specs=in_specs, out_specs=out_specs, check_vma=False)
```

profile of v0, /device:TPU:0, one launch (start us, length us, event | category | flops | bytes accessed | tf_op | source)
XLA Modules:
  0.0 251.6 jit_solution(10912633208323982474)
XLA Ops:
  7.2 0.8 compare_select_fusion
  8.1 0.7 compare_and_fusion
  8.8 0.7 add_convert_fusion.1
  9.5 0.7 broadcast_compare_fusion
  10.2 0.1 reshape.222
  10.3 5.0 %gather_fusion = bf16[14,128]{1,0:T(8,128)(2,1)S(1)} fusion(bf16[32768,128]{1,0:T(8,128)(2,1)} %param.13, s32[1024]{0:T(1024)S(1)} %pad_clamp_fusion), kind=kCustom, calls=%fused_computation | custom fusion | bytes 7224 | tf_op jit(solution)/shard_map/gather | solution.py:65
  15.4 8.3 %psum.28 = bf16[2,7,128]{2,1,0:T(8,128)(2,1)S(1)} all-reduce(bf16[2,7,128]{2,1,0:T(8,128)(2,1)S(1)} %broadcast_select_fusion), channel_id=1, replica_groups=mesh['seq'=4,'tensor'=8] {'seq'}, use_global_device_ids=true, to_apply=%region_0.1 | all-reduce | flops 1792 | bytes 7168 | tf_op jit(solution)/shard_map/psum | solution.py:67
  23.7 26.4 %all_gather.15 = bf16[2,7,1024]{2,1,0:T(8,128)(2,1)S(1)} all-gather(bf16[2,7,128]{2,1,0:T(8,128)(2,1)S(1)} %psum.28), channel_id=1, replica_groups=mesh['seq'=4,'tensor'=8] {'tensor'}, dimensions={2}, use_global_device_ids=true | all-gather | bytes 32256 | tf_op jit(solution)/shard_map/all_gather | solution.py:70
  50.1 0.1 fusion.16
  50.2 1.4 fusion.11
  51.6 0.1 fusion.39
  51.8 0.1 pad_maximum_fusion.1
  51.8 0.8 select_reduce_fusion
  52.6 0.1 copy.53
  52.7 0.2 fusion.23
  53.0 0.1 copy.64
  53.1 5.8 %pmax.7 = f32[2,7,1]{1,0,2:T(2,128)S(1)} all-reduce(f32[2,7,1]{1,0,2:T(2,128)S(1)} %bitcast.154), channel_id=1, replica_groups=mesh['seq'=4,'tensor'=8] {'seq'}, use_global_device_ids=true, to_apply=%region_3.4 | all-reduce | flops 14 | bytes 112 | tf_op jit(solution)/shard_map/pmax | solution.py:106
  58.9 0.1 convolution_multiply_fusion.1
  59.0 0.1 copy.59
  59.1 0.1 fusion.47
  59.3 0.1 copy.63
  59.4 0.1 copy.54
  59.5 2.7 %fusion.6 = f32[2,7,1,128]{3,0,1,2:T(2,128)S(1)} fusion(bf16[7,1280,128]{2,1,0:T(8,128)(2,1)} %param.19, f32[2,7,1,1280]{3,0,1,2:T(2,128)S(1)} %get-tuple-element.74, pred[7,1280]{1,0:T(8,128)(4,1)S(1)} %broadcast_compare_fusion, f32[2,7]{0,1:T(8,128)S(1)} %get-tuple-element.73, f32[2,7]{0,1:T(8,128)S(1)} %copy.54), kind=kOutput, calls=%fused_computation.12 | convolution fusion | flops 27562752 | bytes 2381680 | tf_op jit(solution)/shard_map/sbhj,bjhe->sbhe/dot_general | solution.py:99
  62.2 5.8 %all-reduce.3 = (f32[2,7,1,128]{3,0,1,2:T(2,128)S(1)}, f32[2,7,1]{1,0,2:T(2,128)S(1)}) all-reduce(f32[2,7,1,128]{3,0,1,2:T(2,128)S(1)} %fusion.6, f32[2,7,1]{1,0,2:T(2,128)S(1)} %get-tuple-element.70), channel_id=1, replica_groups=mesh['seq'=4,'tensor'=8] {'seq'}, use_global_device_ids=true, to_apply=%region_4.5 | all-reduce | flops 1806 | bytes 14448 | tf_op jit(solution)/shard_map/psum | solution.py:108
  68.1 0.1 copy.65
  68.2 0.1 copy.60
  68.3 0.2 fusion.10
  68.4 0.8 fusion.13
  69.3 0.8 dynamic_slice.10
  70.1 53.2 %reduce-scatter.3.cloned.1.call-done = f32[2,7,128]{2,1,0:T(8,128)} async-done(((f32[2,7,1024]{2,1,0:T(8,128)}), f32[2,7,128]{2,1,0:T(8,128)}) %reduce-scatter.3.cloned.1.call-update) | async-done | bytes 7184 | tf_op jit(solution)/shard_map/reduce_scatter | solution.py:132
  123.3 0.8 fusion.33
  124.1 7.0 %fusion.62 = f32[14,32768]{1,0:T(8,128)} fusion(bf16[14,128]{1,0:T(8,128)(2,1)S(1)} %reshape.218, bf16[32768,128]{1,0:T(8,128)(2,1)} %param.13), kind=kOutput, calls=%fused_computation.106 | convolution fusion | flops 117440512 | bytes 10227200 | tf_op jit(solution)/shard_map/dot_general | solution.py:141
  131.1 0.1 pad_maximum_fusion
  131.2 0.6 copy.68
  131.8 19.6 %psum.31 = f32[2,7]{1,0:T(2,128)S(1)} all-reduce(f32[2,7]{1,0:T(2,128)S(1)} %get-tuple-element.58), channel_id=1, replica_groups=mesh['seq'=4,'tensor'=8] {'tensor'}, use_global_device_ids=true, to_apply=%region_12.13 | all-reduce | flops 14 | bytes 112 | tf_op jit(solution)/shard_map/psum | solution.py:135
  151.4 0.6 copy.67
  152.0 0.1 mul.205
  152.1 46.9 %reduce-scatter.5.cloned.1.call-done = f32[14,4096]{1,0:T(8,128)} async-done(((f32[14,32768]{1,0:T(8,128)}), f32[14,4096]{1,0:T(8,128)}) %reduce-scatter.5.cloned.1.call-update) | async-done | bytes 229392 | tf_op jit(solution)/shard_map/reduce_scatter | solution.py:145
  199.0 1.2 multiply_reduce_fusion
  200.2 0.2 dynamic-update-slice
  200.4 1.2 exponential_reduce_fusion
  201.6 0.2 dynamic-update-slice.1
  201.9 39.3 %all-reduce.2 = (f32[448]{0:T(512)S(1)}, f32[448]{0:T(512)S(1)}) all-reduce(f32[448]{0:T(512)S(1)} %dynamic-update-slice, f32[448]{0:T(512)S(1)} %dynamic-update-slice.1), channel_id=2, replica_groups=mesh['seq'=4,'tensor'=8] {'seq','tensor'}, use_global_device_ids=true, to_apply=%add | all-reduce | flops 896 | bytes 7168
  241.4 0.1 reshape.236
  241.4 0.1 reshape.237
  241.6 1.2 while.12
  242.8 1.0 multiply_subtract_fusion
  243.9 0.9 copy.69
  (61 shorter events, 1.4 us)
Async XLA Ops:
  7.2 44.7 %copy-start = (bf16[7,1280,128]{2,1,0:T(8,128)(2,1)S(1)}, bf16[7,1280,128]{2,1,0:T(8,128)(2,1)}, u32[]{:S(2)}) copy-start(bf16[7,1280,128]{2,1,0:T(8,128)(2,1)} %param.18) | copy-start | bytes 6881284
  7.2 116.1 %reduce-scatter.3.cloned.1.call-start = ((), (), s32[]{:S(2)}) async-start(), calls=%async_computation.2 | async-start | bytes 73728 | tf_op jit(solution)/shard_map/reduce_scatter | solution.py:132
  51.8 16.6 %copy-start.1 = (bf16[128,1024]{1,0:T(8,128)(2,1)S(1)}, bf16[128,1024]{1,0:T(8,128)(2,1)}, u32[]{:S(2)}) copy-start(bf16[128,1024]{1,0:T(8,128)(2,1)} %param.17) | copy-start | bytes 786436
  69.3 129.8 %reduce-scatter.5.cloned.1.call-start = ((), (), s32[]{:S(2)}) async-start(), calls=%async_computation.3 | async-start | bytes 2359296 | tf_op jit(solution)/shard_map/reduce_scatter | solution.py:145
Sparse Core Ops, SparseCore 0:
  69.4 53.8 reduce-scatter.2
  131.3 67.7 reduce-scatter.4
where the time goes:
time: 252 us
  blocking collectives  105 us (42%)
  waiting for transfers between devices  100 us (40%)
  between operations  14.2 us (6%)
  matrix products  13 us (5%)
  local copies, waits for them, and re-layouts  9.57 us (4%)
  other arithmetic  8.84 us (4%)
    reduce_scatter x1, waiting for transfers between devices, body(): lax.psum_scatter(mixed_rows, 'tensor', scatter_dimension=2, tiled=True)  53.2 us
    reduce_scatter x1, waiting for transfers between devices, body(): lax.psum_scatter(partial_logits, 'tensor', scatter_dimension=1, tiled=True)  46.9 us
    unnamed x1, blocking collectives  39.3 us
    all_gather x1, blocking collectives, body(): lax.all_gather(embed_local.astype(jnp.bfloat16), 'tensor', axis=2, tiled=...  26.4 us
    psum x1, blocking collectives, body(): final_squares = lax.psum(jnp.sum(hidden_float * hidden_float, -1), 'tensor')  19.6 us
    psum x1, blocking collectives, body(): lax.psum(picked.astype(jnp.float32).astype(jnp.bfloat16), 'seq')  8.35 us
    dot_general x1, matrix products, body(): lax.dot_general(gated_rows, embed_table, (((1,), (1,)), ((), ())), prefer...  7.03 us
    pmax x1, blocking collectives, body(): highest = lax.pmax(local_max, 'seq')  5.85 us
  transfers between devices with their start and end apart: 2, of which 2 were waited for; matrix products, arithmetic and copies ran while one was open for 1% of the time, Pallas kernels for 0%

commit v1 on v0

--- a/solution.py
+++ b/solution.py
@@ -67,8 +67,11 @@
     embed_local = lax.psum(picked.astype(jnp.float32).astype(jnp.bfloat16), "seq").astype(
         jnp.float32
     )
-    embed_whole = lax.all_gather(
-        embed_local.astype(jnp.bfloat16), "tensor", axis=2, tiled=True
+    embed_whole = jnp.concatenate(
+        lax.all_to_all(
+            jnp.stack([embed_local.astype(jnp.bfloat16)] * lax.axis_size("tensor")), "tensor", 0, 0
+        ),
+        axis=2,
     ).astype(jnp.float32)
     normed = (
         embed_whole

time: 252 us -> 236 us (0.937)
  blocking collectives: 105 us -> 79.1 us
  starting transfers between devices: 0.08 us -> 5.91 us
  waiting for transfers between devices: 100 us -> 103 us
    all_gather x1 -> x0, blocking collectives: 26.4 us -> none  [body(): lax.all_gather(embed_local.astype(jnp.bfloat16), 'tensor', axis=2, tiled=...]
    all_to_all x0 -> x1, starting transfers between devices: none -> 5.83 us  [body(): lax.all_to_all(jnp.stack([embed_local.astype(jnp.bfloat16)] * lax.axis_si...]
    all_to_all x0 -> x1, waiting for transfers between devices: none -> 5.18 us  [body(): lax.all_to_all(jnp.stack([embed_local.astype(jnp.bfloat16)] * lax.axis_si...]
  transfers between devices with their start and end apart: 2 -> 3, of which waited for: 2 -> 3; matrix products, arithmetic and copies ran while one was open for 1% -> 2% of each run, Pallas kernels for 0% -> 0%
where the time goes in v1:
time: 236 us
  waiting for transfers between devices  103 us (44%)
  blocking collectives  79.1 us (34%)
  between operations  14.2 us (6%)
  matrix products  13 us (6%)
  local copies, waits for them, and re-layouts  10.5 us (4%)
  other arithmetic  9.67 us (4%)
  starting transfers between devices  5.91 us (3%)
    reduce_scatter x1, waiting for transfers between devices, body(): lax.psum_scatter(mixed_rows, 'tensor', scatter_dimension=2, tiled=True)  51.1 us
    reduce_scatter x1, waiting for transfers between devices, body(): lax.psum_scatter(partial_logits, 'tensor', scatter_dimension=1, tiled=True)  46.6 us
    unnamed x1, blocking collectives  39.5 us
    psum x1, blocking collectives, body(): final_squares = lax.psum(jnp.sum(hidden_float * hidden_float, -1), 'tensor')  19.6 us
    psum x1, blocking collectives, body(): lax.psum(picked.astype(jnp.float32).astype(jnp.bfloat16), 'seq')  8.35 us
    dot_general x1, matrix products, body(): lax.dot_general(gated_rows, embed_table, (((1,), (1,)), ((), ())), prefer...  7.03 us
    pmax x1, blocking collectives, body(): highest = lax.pmax(local_max, 'seq')  5.85 us
    psum x1, blocking collectives, body(): lax.psum((local_sum * factor, local_out * factor[..., None]), 'seq')  5.85 us
  transfers between devices with their start and end apart: 3, of which 3 were waited for; matrix products, arithmetic and copies ran while one was open for 2% of the time, Pallas kernels for 0%

profile of v1, /device:TPU:0, one launch (start us, length us, event | category | flops | bytes accessed | tf_op | source)
XLA Modules:
  0.0 235.8 jit_solution(16338843730519222198)
XLA Ops:
  7.2 0.8 compare_select_fusion
  8.0 0.7 compare_and_fusion
  8.8 5.0 %gather_fusion = bf16[14,128]{1,0:T(8,128)(2,1)S(1)} fusion(bf16[32768,128]{1,0:T(8,128)(2,1)} %param.13, s32[1024]{0:T(1024)S(1)} %pad_clamp_fusion), kind=kCustom, calls=%fused_computation | custom fusion | bytes 7224 | tf_op jit(solution)/shard_map/gather | solution.py:65
  13.9 8.3 %psum.28 = bf16[2,7,128]{2,1,0:T(8,128)(2,1)S(1)} all-reduce(bf16[2,7,128]{2,1,0:T(8,128)(2,1)S(1)} %broadcast_select_fusion), channel_id=1, replica_groups=mesh['seq'=4,'tensor'=8] {'seq'}, use_global_device_ids=true, to_apply=%region_0.1 | all-reduce | flops 1792 | bytes 7168 | tf_op jit(solution)/shard_map/psum | solution.py:67
  22.3 0.6 stack.4
  22.9 5.8 %all-to-all-start = ((bf16[8,2,7,128]{3,1,2,0:T(2,128)(2,1)}), bf16[8,2,7,128]{3,1,2,0:T(2,128)(2,1)S(1)}, u32[]{:S(2)}, u32[]{:S(2)}) async-start(bf16[8,2,7,128]{3,1,2,0:T(2,128)(2,1)} %stack.4), calls=%async_computation | async-start | bytes 57344 | tf_op jit(solution)/shard_map/all_to_all | solution.py:71
  28.8 0.7 add_convert_fusion.1
  29.5 0.7 broadcast_compare_fusion
  30.2 5.2 %all-to-all-done = bf16[8,2,7,128]{3,1,2,0:T(2,128)(2,1)S(1)} async-done(((bf16[8,2,7,128]{3,1,2,0:T(2,128)(2,1)}), bf16[8,2,7,128]{3,1,2,0:T(2,128)(2,1)S(1)}, u32[]{:S(2)}, u32[]{:S(2)}) %all-to-all-start) | async-done | bytes 28704 | tf_op jit(solution)/shard_map/all_to_all | solution.py:71
  35.4 0.1 fusion.16
  35.5 0.1 copy.137
  35.7 0.8 fusion.20
  36.5 1.4 fusion.11
  37.8 0.1 fusion.37
  38.0 0.8 select_reduce_fusion
  38.8 0.1 copy.112
  38.9 0.2 fusion.21
  39.2 0.1 copy.123
  39.3 5.8 %pmax.7 = f32[2,7,1]{1,0,2:T(2,128)S(1)} all-reduce(f32[2,7,1]{1,0,2:T(2,128)S(1)} %bitcast.155), channel_id=1, replica_groups=mesh['seq'=4,'tensor'=8] {'seq'}, use_global_device_ids=true, to_apply=%region_3.4 | all-reduce | flops 14 | bytes 112 | tf_op jit(solution)/shard_map/pmax | solution.py:109
  45.1 0.1 convolution_multiply_fusion.1
  45.2 0.1 copy.118
  45.5 0.1 copy.122
  45.6 0.1 copy.113
  45.7 2.7 %fusion.6 = f32[2,7,1,128]{3,0,1,2:T(2,128)S(1)} fusion(bf16[7,1280,128]{2,1,0:T(8,128)(2,1)} %param.19, f32[2,7,1,1280]{3,0,1,2:T(2,128)S(1)} %get-tuple-element.80, pred[7,1280]{1,0:T(8,128)(4,1)S(1)} %broadcast_compare_fusion, f32[2,7]{0,1:T(8,128)S(1)} %get-tuple-element.79, f32[2,7]{0,1:T(8,128)S(1)} %copy.113), kind=kOutput, calls=%fused_computation.12 | convolution fusion | flops 27562752 | bytes 2381680 | tf_op jit(solution)/shard_map/sbhj,bjhe->sbhe/dot_general | solution.py:102
  48.4 5.8 %all-reduce.3 = (f32[2,7,1,128]{3,0,1,2:T(2,128)S(1)}, f32[2,7,1]{1,0,2:T(2,128)S(1)}) all-reduce(f32[2,7,1,128]{3,0,1,2:T(2,128)S(1)} %fusion.6, f32[2,7,1]{1,0,2:T(2,128)S(1)} %get-tuple-element.76), channel_id=1, replica_groups=mesh['seq'=4,'tensor'=8] {'seq'}, use_global_device_ids=true, to_apply=%region_4.5 | all-reduce | flops 1806 | bytes 14448 | tf_op jit(solution)/shard_map/psum | solution.py:111
  54.3 0.1 copy.124
  54.4 0.1 copy.119
  54.5 0.2 fusion.10
  54.6 0.8 fusion.13
  55.5 0.8 dynamic_slice.10
  56.3 51.1 %reduce-scatter.3.cloned.1.call-done = f32[2,7,128]{2,1,0:T(8,128)} async-done(((f32[2,7,1024]{2,1,0:T(8,128)}), f32[2,7,128]{2,1,0:T(8,128)}) %reduce-scatter.3.cloned.1.call-update) | async-done | bytes 7184 | tf_op jit(solution)/shard_map/reduce_scatter | solution.py:135
  107.4 0.8 fusion.31
  108.2 7.0 %fusion.60 = f32[14,32768]{1,0:T(8,128)} fusion(bf16[14,128]{1,0:T(8,128)(2,1)S(1)} %reshape.224, bf16[32768,128]{1,0:T(8,128)(2,1)} %param.13), kind=kOutput, calls=%fused_computation.106 | convolution fusion | flops 117440512 | bytes 10227200 | tf_op jit(solution)/shard_map/dot_general | solution.py:144
  115.4 0.6 copy.129
  116.0 19.6 %psum.31 = f32[2,7]{0,1:T(8,128)S(1)} all-reduce(f32[2,7]{0,1:T(8,128)S(1)} %copy.126), channel_id=1, replica_groups=mesh['seq'=4,'tensor'=8] {'tensor'}, use_global_device_ids=true, to_apply=%region_12.13 | all-reduce | flops 14 | bytes 112 | tf_op jit(solution)/shard_map/psum | solution.py:138
  135.6 0.6 copy.128
  136.2 0.1 copy.127
  136.4 46.6 %reduce-scatter.5.cloned.1.call-done = f32[14,4096]{1,0:T(8,128)} async-done(((f32[14,32768]{1,0:T(8,128)}), f32[14,4096]{1,0:T(8,128)}) %reduce-scatter.5.cloned.1.call-update) | async-done | bytes 229392 | tf_op jit(solution)/shard_map/reduce_scatter | solution.py:148
  183.0 1.2 multiply_reduce_fusion
  184.2 0.2 dynamic-update-slice
  184.4 1.2 exponential_reduce_fusion
  185.6 0.2 dynamic-update-slice.1
  185.8 39.5 %all-reduce.2 = (f32[448]{0:T(512)S(1)}, f32[448]{0:T(512)S(1)}) all-reduce(f32[448]{0:T(512)S(1)} %dynamic-update-slice, f32[448]{0:T(512)S(1)} %dynamic-update-slice.1), channel_id=2, replica_groups=mesh['seq'=4,'tensor'=8] {'seq','tensor'}, use_global_device_ids=true, to_apply=%add | all-reduce | flops 896 | bytes 7168
  225.5 0.1 reshape.243
  225.6 0.1 reshape.244
  225.7 1.2 while.12
  227.0 1.0 multiply_subtract_fusion
  228.1 0.9 copy.130
  (70 shorter events, 1.9 us)
Async XLA Ops:
  7.2 30.9 %copy-start = (bf16[7,1280,128]{2,1,0:T(8,128)(2,1)S(1)}, bf16[7,1280,128]{2,1,0:T(8,128)(2,1)}, u32[]{:S(2)}) copy-start(bf16[7,1280,128]{2,1,0:T(8,128)(2,1)} %param.18) | copy-start | bytes 6881284
  22.9 12.5 %all-to-all-start = ((bf16[8,2,7,128]{3,1,2,0:T(2,128)(2,1)}), bf16[8,2,7,128]{3,1,2,0:T(2,128)(2,1)S(1)}, u32[]{:S(2)}, u32[]{:S(2)}) async-start(bf16[8,2,7,128]{3,1,2,0:T(2,128)(2,1)} %stack.4), calls=%async_computation | async-start | bytes 57344 | tf_op jit(solution)/shard_map/all_to_all | solution.py:71
  28.7 78.7 %reduce-scatter.3.cloned.1.call-start = ((), (), s32[]{:S(2)}) async-start(), calls=%async_computation.3 | async-start | bytes 73728 | tf_op jit(solution)/shard_map/reduce_scatter | solution.py:135
  38.0 16.6 %copy-start.1 = (bf16[128,1024]{1,0:T(8,128)(2,1)S(1)}, bf16[128,1024]{1,0:T(8,128)(2,1)}, u32[]{:S(2)}) copy-start(bf16[128,1024]{1,0:T(8,128)(2,1)} %param.17) | copy-start | bytes 786436
  55.4 127.6 %reduce-scatter.5.cloned.1.call-start = ((), (), s32[]{:S(2)}) async-start(), calls=%async_computation.4 | async-start | bytes 2359296 | tf_op jit(solution)/shard_map/reduce_scatter | solution.py:148
Sparse Core Ops, SparseCore 0:
  55.6 51.7 reduce-scatter.2
  115.4 67.5 reduce-scatter.4
